TPU v7x, 256 devices: a whole 4x4x8 slice. The times are simulated.
256 devices in a mesh: unit: 4 (over y), bank: 4 (over x), zero: 16 (over z, core).
Axes of the slice: x: 4, y: 4, z: 8, core: 2. Of those that a mesh axis runs over, the one named last changes fastest.
Arguments:
- train_down: float32 [256, 1024, 2048], P(('unit', 'bank'), None, 'zero'), parts along dimension 0, may hold values from -0.25 to 0.25
- router_weight: float32 [8192, 64], P(('unit', 'zero'), 'bank'), parts along dimension 0, may hold values from -0.125 to 0.125
- router_gain: float32 [8192], P(('unit', 'zero')), parts along dimension 0, may hold values from 0.25 to 1.75
Outputs:
- ready_down: bfloat16 [256, 1024, 2048], P(('unit', 'bank'), 'zero'), parts along dimension 0
- scale_down: float32 [256, 1024], P(('unit', 'bank'), 'zero'), parts along dimension 0
- serve_router: bfloat16 [8192, 64], P('unit'), parts along dimension 0
There are 4 independent parts, one for each index of `unit`. A program takes and returns all parts, laid end to end along the dimension named above; each array names one. Nothing has to cross between parts.
All inputs are finite; a program needn't handle non-finite values.
Results may differ from a plain program's by a relative error of at most 0.001.
Values may be sent and summed in bfloat16 or wider, within the bound.
A program may use at most 128 MiB of HBM per device.

v0:
```python
import jax
import jax.numpy as jnp
from jax import lax
from jax.sharding import Mesh
from jax.sharding import PartitionSpec as P

ZERO = ("zero_0", "zero_1")
UNIT_ZERO = ("unit", "zero_0", "zero_1")


def gathered_total(value, axis):
    tiles = lax.all_gather(value, axis)
    return tiles.max(axis=0)


def in_blocks(value, dim, length):
    return jnp.stack(jnp.split(value, length, axis=dim))


def joined_along(tiles, dim):
    tiles = jnp.moveaxis(tiles, 0, dim)
    dims = tiles.shape
    return tiles.reshape(*dims[:dim], dims[dim] * dims[dim + 1], *dims[dim + 2 :])


def turned_blocks(tiles, axes, sequence):
    dims = [lax.axis_size(a) for a in axes]
    tiles = tiles.reshape(*dims, *tiles.shape[1:])
    for k in sequence:
        tiles = lax.all_to_all(tiles, axes[k], split_axis=k, concat_axis=k, tiled=True)
    return tiles.reshape(-1, *tiles.shape[len(axes) :])


def two_step_exchange(value, groups, sequence, split_dim, concat_dim):
    length = lax.axis_size(groups[0]) * lax.axis_size(groups[1])
    tiles = in_blocks(value, split_dim, length)
    return joined_along(turned_blocks(tiles, groups, sequence), concat_dim)


def per_device(train_down, router_weight, router_gain):
    scale_down = gathered_total(jnp.max(jnp.abs(train_down), axis=2), ZERO)
    narrow_down = (train_down / jnp.expand_dims(scale_down, 2)).astype(jnp.bfloat16)
    ready_down = two_step_exchange(narrow_down, ("zero_0", "zero_1"), (1, 0), 1, 2)
    scale_down = lax.dynamic_slice_in_dim(
        scale_down, lax.axis_index(ZERO) * ready_down.shape[1], ready_down.shape[1], axis=1
    )
    part_router = (router_weight * router_gain[:, None]).astype(jnp.bfloat16)
    row_router = lax.all_gather(part_router, ZERO, axis=0, tiled=True)
    serve_router = lax.all_gather(row_router, "bank", axis=1, tiled=True)
    return (ready_down, scale_down, serve_router)


def solution(mesh):
    torus = Mesh(
        mesh.devices.reshape(mesh.shape["unit"], mesh.shape["bank"], 8, 2),
        ("unit", "bank", "zero_0", "zero_1"),
    )
    placed = (P(("unit", "bank"), None, ZERO), P(UNIT_ZERO, "bank"), P(UNIT_ZERO))
    return jax.shard_map(
        per_device,
        mesh=torus,
        in_specs=placed,
        out_specs=(P(("unit", "bank"), ZERO, None), P(("unit", "bank"), ZERO), P("unit", None)),
        check_vma=False,
    )
```

profile of v0, /device:TPU:2, one launch (start us, length us, event | category | flops | bytes accessed | tf_op | source)
XLA Modules:
  0.0 208.9 jit_solution(14406718394577058157)
XLA Ops:
  7.2 0.0 all-gather.3.cloned.1.call-start
  7.2 6.2 %abs_reduce_fusion = f32[16,1024]{1,0:T(8,128)} fusion(f32[16,1024,128]{2,1,0:T(8,128)} %param.3), kind=kLoop, calls=%fused_computation.1 | loop fusion | flops 4177920 | bytes 8454144 | tf_op jit(solution)/shard_map/reduce_max | solution.py:41
  13.5 0.0 all-gather.3.cloned.1.call-update
  13.5 41.7 %all-gather.3.cloned.1.call-done = f32[256,1024]{1,0:T(8,128)} async-done(((f32[16,1024]{1,0:T(8,128)}), f32[256,1024]{1,0:T(8,128)}) %all-gather.3.cloned.1.call-update) | async-done | bytes 1048592 | tf_op jit(solution)/shard_map/all_gather | solution.py:12
  55.1 1.3 reduce_max.19
  56.4 5.3 %divide_convert_fusion = bf16[16,1024,128]{2,1,0:T(8,128)(2,1)S(1)} fusion(f32[16,1024,128]{2,1,0:T(8,128)} %param.3, f32[16,1024]{1,0:T(8,128)S(1)} %reduce_max.19), kind=kLoop, calls=%fused_computation | loop fusion | flops 4194304 | bytes 12648448 | tf_op jit(solution)/shard_map/convert_element_type | solution.py:42
  62.4 1.3 copy.12
  63.7 7.1 %all_to_all.10 = bf16[8,2,16,64,128]{4,3,2,0,1:T(8,128)(2,1)S(1)} all-to-all(bf16[8,2,16,64,128]{4,3,2,0,1:T(8,128)(2,1)S(1)} %copy.12), channel_id=1, replica_groups=mesh['unit'=4,'bank'=4,'zero_0'=8,'zero_1'=2] {'zero_1'}, dimensions={1} | all-to-all | bytes 8388608 | tf_op jit(solution)/shard_map/all_to_all | solution.py:30
  70.8 3.0 %copy.13 = bf16[8,2,16,64,128]{4,3,2,1,0:T(8,128)(2,1)} copy(bf16[8,2,16,64,128]{4,3,2,0,1:T(8,128)(2,1)S(1)} %all_to_all.10) | data formatting | bytes 8388608 | tf_op jit(solution)/shard_map/all_to_all | solution.py:30
  73.8 0.0 copy-start
  73.8 0.0 copy-start.1
  73.8 4.7 %all-to-all-start.1 = ((bf16[8,2,16,64,128]{4,3,2,1,0:T(8,128)(2,1)}), bf16[8,2,16,64,128]{4,3,2,1,0:T(8,128)(2,1)}, u32[]{:S(2)}, u32[]{:S(2)}) async-start(bf16[8,2,16,64,128]{4,3,2,1,0:T(8,128)(2,1)} %copy.13), calls=%async_computation.1 | async-start | bytes 8388608 | tf_op jit(solution)/shard_map/all_to_all | solution.py:30
  78.5 0.0 copy-done
  78.5 0.0 copy-done.1
  78.5 104.4 %all_gather.14 = bf16[2048,16]{0,1:T(8,128)(2,1)S(1)} all-gather(bf16[128,16]{0,1:T(8,128)(2,1)S(1)} %multiply_convert_fusion), channel_id=1, replica_groups=mesh['unit'=4,'bank'=4,'zero_0'=8,'zero_1'=2] {'zero_0','zero_1'}, dimensions={0}, use_global_device_ids=true | all-gather | bytes 69632 | tf_op jit(solution)/shard_map/all_gather | solution.py:48
  182.9 12.5 %all_gather.15 = bf16[2048,64]{0,1:T(8,128)(2,1)S(1)} all-gather(bf16[2048,16]{0,1:T(8,128)(2,1)S(1)} %all_gather.14), channel_id=1, replica_groups=mesh['unit'=4,'bank'=4,'zero_0'=8,'zero_1'=2] {'bank'}, dimensions={1}, use_global_device_ids=true | all-gather | bytes 327680 | tf_op jit(solution)/shard_map/all_gather | solution.py:49
  195.4 0.7 constant_dynamic-slice_fusion
  196.0 0.0 all-to-all-done.1
  196.0 5.3 %copy.17 = bf16[16,16,8,8,128]{4,3,0,2,1:T(8,128)(2,1)} copy(bf16[16,16,8,8,128]{4,3,2,1,0:T(8,128)(2,1)} %bitcast.21) | data formatting | bytes 8388608 | tf_op jit(solution)/shard_map/reshape | solution.py:23
  201.4 0.7 copy.34
  (17 shorter events, 0.6 us)
Async XLA Ops:
  7.2 48.0 %all-gather.3.cloned.1.call-start = ((), (), s32[]{:S(2)}) async-start(), calls=%async_computation.2 | async-start | bytes 1114112 | tf_op jit(solution)/shard_map/all_gather | solution.py:12
  73.8 4.7 %copy-start = (f32[128,16]{0,1:T(8,128)S(1)}, f32[128,16]{0,1:T(8,128)}, u32[]{:S(2)}) copy-start(f32[128,16]{0,1:T(8,128)} %param.4) | copy-start | bytes 24580
  73.8 4.7 %copy-start.1 = (f32[128]{0:T(128)S(1)}, f32[128]{0:T(128)}, u32[]{:S(2)}) copy-start(f32[128]{0:T(128)} %param.5) | copy-start | bytes 1540
  73.8 122.2 %all-to-all-start.1 = ((bf16[8,2,16,64,128]{4,3,2,1,0:T(8,128)(2,1)}), bf16[8,2,16,64,128]{4,3,2,1,0:T(8,128)(2,1)}, u32[]{:S(2)}, u32[]{:S(2)}) async-start(bf16[8,2,16,64,128]{4,3,2,1,0:T(8,128)(2,1)} %copy.13), calls=%async_computation.1 | async-start | bytes 8388608 | tf_op jit(solution)/shard_map/all_to_all | solution.py:30
Sparse Core Ops, SparseCore 0:
  13.6 41.4 all-gather.2
where the time goes:
time: 209 us
  blocking collectives  124 us (59%)
  waiting for transfers between devices  41.7 us (20%)
  between operations  14.2 us (7%)
  other arithmetic  12.8 us (6%)
  local copies, waits for them, and re-layouts  11.6 us (6%)
  starting transfers between devices  4.71 us (2%)
    all_gather x1, blocking collectives, per_device(): row_router = lax.all_gather(part_router, ZERO, axis=0, tiled=True)  104 us
    all_gather x1, waiting for transfers between devices, gathered_total(): tiles = lax.all_gather(value, axis)  41.7 us
    all_gather x1, blocking collectives, per_device(): serve_router = lax.all_gather(row_router, 'bank', axis=1, tiled=True)  12.5 us
    all_to_all x1, blocking collectives, turned_blocks(): lax.all_to_all(tiles, axes[k], split_axis=k, concat_axis=k, tiled=True)  7.1 us
    reduce_max x1, other arithmetic, per_device(): scale_down = gathered_total(jnp.max(jnp.abs(train_down), axis=2), ZERO)  6.25 us
    reshape x1, local copies, waits for them, and re-layouts, joined_along(): tiles.reshape(*dims[:dim], dims[dim] * dims[dim + 1], *dims[dim + 2:])  5.35 us
    convert_element_type x1, other arithmetic, per_device(): (train_down / jnp.expand_dims(scale_down, 2)).astype(jnp.bfloat16)  5.26 us
    all_to_all x1, starting transfers between devices, turned_blocks(): lax.all_to_all(tiles, axes[k], split_axis=k, concat_axis=k, tiled=True)  4.67 us
  transfers between devices with their start and end apart: 2, of which 1 were waited for; matrix products, arithmetic and copies ran while one was open for 0% of the time, Pallas kernels for 0%

commit v1 on v0

--- a/solution.py
+++ b/solution.py
@@ -6,6 +6,14 @@
 
 ZERO = ("zero_0", "zero_1")
 UNIT_ZERO = ("unit", "zero_0", "zero_1")
+
+
+def gather_by_exchange(array, axis, dim):
+    size = lax.axis_size(axis)
+    repeats = [size if d == dim else 1 for d in range(array.ndim)]
+    return lax.all_to_all(
+        jnp.tile(array, repeats), axis, split_axis=dim, concat_axis=dim, tiled=True
+    )
 
 
 def gathered_total(value, axis):
@@ -46,7 +54,7 @@
     )
     part_router = (router_weight * router_gain[:, None]).astype(jnp.bfloat16)
     row_router = lax.all_gather(part_router, ZERO, axis=0, tiled=True)
-    serve_router = lax.all_gather(row_router, "bank", axis=1, tiled=True)
+    serve_router = gather_by_exchange(row_router, "bank", 1)
     return (ready_down, scale_down, serve_router)
 
 

time: 209 us -> 198 us (0.947)
  blocking collectives: 124 us -> 28.3 us
  waiting for transfers between devices: 41.7 us -> 117 us
  starting transfers between devices: 4.71 us -> 9.39 us
  local copies, waits for them, and re-layouts: 11.6 us -> 14.8 us
    all_to_all x1, waiting for transfers between devices: 0.01 us -> 95.6 us  [turned_blocks(): lax.all_to_all(tiles, axes[k], split_axis=k, concat_axis=k, tiled=True)]
    all_gather x1, blocking collectives: 104 us -> 20.1 us  [per_device(): row_router = lax.all_gather(part_router, ZERO, axis=0, tiled=True)]
    all_gather x1, waiting for transfers between devices: 41.7 us -> 21.5 us  [gathered_total(): tiles = lax.all_gather(value, axis)]
    all_gather x1 -> x0, blocking collectives: 12.5 us -> none  [per_device(): serve_router = lax.all_gather(row_router, 'bank', axis=1, tiled=True)]
    all_to_all x0 -> x1, starting transfers between devices: none -> 4.8 us  [gather_by_exchange(): lax.all_to_all(jnp.tile(array, repeats), axis, split_axis=dim, concat_axi...]
    all_to_all x1, local copies, waits for them, and re-layouts: 2.97 us -> 5.52 us  [turned_blocks(): lax.all_to_all(tiles, axes[k], split_axis=k, concat_axis=k, tiled=True)]
  transfers between devices with their start and end apart: 2 -> 3, of which waited for: 1 -> 2; matrix products, arithmetic and copies ran while one was open for 0% -> 3% of each run, Pallas kernels for 0% -> 0%
where the time goes in v1:
time: 198 us; the launch traced here: 197 us
  waiting for transfers between devices  117 us (59%)
  blocking collectives  28.3 us (14%)
  local copies, waits for them, and re-layouts  14.8 us (7%)
  between operations  14.2 us (7%)
  other arithmetic  12.8 us (6%)
  starting transfers between devices  9.39 us (5%)
    all_to_all x1, waiting for transfers between devices, turned_blocks(): lax.all_to_all(tiles, axes[k], split_axis=k, concat_axis=k, tiled=True)  95.6 us
    all_gather x1, waiting for transfers between devices, gathered_total(): tiles = lax.all_gather(value, axis)  21.5 us
    all_gather x1, blocking collectives, per_device(): row_router = lax.all_gather(part_router, ZERO, axis=0, tiled=True)  20.1 us
    all_to_all x1, blocking collectives, turned_blocks(): lax.all_to_all(tiles, axes[k], split_axis=k, concat_axis=k, tiled=True)  8.15 us
    reduce_max x1, other arithmetic, per_device(): scale_down = gathered_total(jnp.max(jnp.abs(train_down), axis=2), ZERO)  6.25 us
    all_to_all x1, local copies, waits for them, and re-layouts, turned_blocks(): lax.all_to_all(tiles, axes[k], split_axis=k, concat_axis=k, tiled=True)  5.52 us
    reshape x1, local copies, waits for them, and re-layouts, joined_along(): tiles.reshape(*dims[:dim], dims[dim] * dims[dim + 1], *dims[dim + 2:])  5.35 us
    convert_element_type x1, other arithmetic, per_device(): (train_down / jnp.expand_dims(scale_down, 2)).astype(jnp.bfloat16)  5.26 us
  transfers between devices with their start and end apart: 3, of which 2 were waited for; matrix products, arithmetic and copies ran while one was open for 3% of the time, Pallas kernels for 0%

profile of v1, /device:TPU:2, one launch (start us, length us, event | category | flops | bytes accessed | tf_op | source)
XLA Modules:
  0.0 196.6 jit_solution(3755257042915347789)
XLA Ops:
  7.2 0.0 copy-start
  7.2 0.0 copy-start.1
  7.2 0.0 all-gather.3.cloned.1.call-start
  7.2 6.2 %abs_reduce_fusion = f32[16,1024]{1,0:T(8,128)} fusion(f32[16,1024,128]{2,1,0:T(8,128)} %param.3), kind=kLoop, calls=%fused_computation.1 | loop fusion | flops 4177920 | bytes 8454144 | tf_op jit(solution)/shard_map/reduce_max | solution.py:49
  13.5 0.0 all-gather.3.cloned.1.call-update
  13.5 0.0 copy-done
  13.5 0.0 copy-done.1
  13.5 20.1 %all_gather.11 = bf16[2048,16]{0,1:T(8,128)(2,1)S(1)} all-gather(bf16[128,16]{0,1:T(8,128)(2,1)S(1)} %multiply_convert_fusion), channel_id=1, replica_groups=mesh['unit'=4,'bank'=4,'zero_0'=8,'zero_1'=2] {'zero_0','zero_1'}, dimensions={0}, use_global_device_ids=true | all-gather | bytes 69632 | tf_op jit(solution)/shard_map/all_gather | solution.py:56
  33.7 21.5 %all-gather.3.cloned.1.call-done = f32[256,1024]{1,0:T(8,128)} async-done(((f32[16,1024]{1,0:T(8,128)}), f32[256,1024]{1,0:T(8,128)}) %all-gather.3.cloned.1.call-update) | async-done | bytes 1048592 | tf_op jit(solution)/shard_map/all_gather | solution.py:20
  55.2 1.3 reduce_max.19
  56.5 5.3 %divide_convert_fusion = bf16[16,1024,128]{2,1,0:T(8,128)(2,1)S(1)} fusion(f32[16,1024,128]{2,1,0:T(8,128)} %param.3, f32[16,1024]{1,0:T(8,128)S(1)} %reduce_max.19), kind=kLoop, calls=%fused_computation | loop fusion | flops 4194304 | bytes 12648448 | tf_op jit(solution)/shard_map/convert_element_type | solution.py:50
  62.4 1.3 copy.12
  63.7 8.2 %all_to_all.19 = bf16[8,2,16,64,128]{4,3,2,0,1:T(8,128)(2,1)} all-to-all(bf16[8,2,16,64,128]{4,3,2,0,1:T(8,128)(2,1)S(1)} %copy.12), channel_id=1, replica_groups=mesh['unit'=4,'bank'=4,'zero_0'=8,'zero_1'=2] {'zero_1'}, dimensions={1} | all-to-all | bytes 8388608 | tf_op jit(solution)/shard_map/all_to_all | solution.py:38
  71.9 0.7 tile.2
  72.6 4.8 %all-to-all-start.2 = ((bf16[2048,4,16]{0,2,1:T(8,128)(2,1)}), bf16[2048,4,16]{0,2,1:T(8,128)(2,1)S(1)}, u32[]{:S(2)}, u32[]{:S(2)}) async-start(bf16[2048,4,16]{0,2,1:T(8,128)(2,1)} %tile.2), calls=%async_computation.2 | async-start | bytes 524288 | tf_op jit(solution)/shard_map/all_to_all | solution.py:14
  77.4 5.5 %copy.13 = bf16[8,2,16,64,128]{4,3,2,1,0:T(8,128)(2,1)} copy(bf16[8,2,16,64,128]{4,3,2,0,1:T(8,128)(2,1)} %all_to_all.19) | data formatting | bytes 8388608 | tf_op jit(solution)/shard_map/all_to_all | solution.py:38
  82.9 0.0 all-to-all-done.2
  82.9 4.5 %all-to-all-start.1 = ((bf16[8,2,16,64,128]{4,3,2,1,0:T(8,128)(2,1)}), bf16[8,2,16,64,128]{4,3,2,1,0:T(8,128)(2,1)}, u32[]{:S(2)}, u32[]{:S(2)}) async-start(bf16[8,2,16,64,128]{4,3,2,1,0:T(8,128)(2,1)} %copy.13), calls=%async_computation.1 | async-start | bytes 8388608 | tf_op jit(solution)/shard_map/all_to_all | solution.py:38
  87.5 0.7 constant_dynamic-slice_fusion
  88.2 95.6 %all-to-all-done.1 = bf16[8,2,16,64,128]{4,3,2,1,0:T(8,128)(2,1)} async-done(((bf16[8,2,16,64,128]{4,3,2,1,0:T(8,128)(2,1)}), bf16[8,2,16,64,128]{4,3,2,1,0:T(8,128)(2,1)}, u32[]{:S(2)}, u32[]{:S(2)}) %all-to-all-start.1) | async-done | bytes 4194336 | tf_op jit(solution)/shard_map/all_to_all | solution.py:38
  183.7 5.3 %copy.17 = bf16[16,16,8,8,128]{4,3,0,2,1:T(8,128)(2,1)} copy(bf16[16,16,8,8,128]{4,3,2,1,0:T(8,128)(2,1)} %bitcast.22) | data formatting | bytes 8388608 | tf_op jit(solution)/shard_map/reshape | solution.py:31
  189.1 0.7 copy.34
  (17 shorter events, 0.6 us)
Async XLA Ops:
  7.2 6.3 %copy-start = (f32[128,16]{0,1:T(8,128)S(1)}, f32[128,16]{0,1:T(8,128)}, u32[]{:S(2)}) copy-start(f32[128,16]{0,1:T(8,128)} %param.4) | copy-start | bytes 24580
  7.2 6.3 %copy-start.1 = (f32[128]{0:T(128)S(1)}, f32[128]{0:T(128)}, u32[]{:S(2)}) copy-start(f32[128]{0:T(128)} %param.5) | copy-start | bytes 1540
  7.2 48.0 %all-gather.3.cloned.1.call-start = ((), (), s32[]{:S(2)}) async-start(), calls=%async_computation.3 | async-start | bytes 1114112 | tf_op jit(solution)/shard_map/all_gather | solution.py:20
  72.6 10.3 %all-to-all-start.2 = ((bf16[2048,4,16]{0,2,1:T(8,128)(2,1)}), bf16[2048,4,16]{0,2,1:T(8,128)(2,1)S(1)}, u32[]{:S(2)}, u32[]{:S(2)}) async-start(bf16[2048,4,16]{0,2,1:T(8,128)(2,1)} %tile.2), calls=%async_computation.2 | async-start | bytes 524288 | tf_op jit(solution)/shard_map/all_to_all | solution.py:14
  82.9 100.8 %all-to-all-start.1 = ((bf16[8,2,16,64,128]{4,3,2,1,0:T(8,128)(2,1)}), bf16[8,2,16,64,128]{4,3,2,1,0:T(8,128)(2,1)}, u32[]{:S(2)}, u32[]{:S(2)}) async-start(bf16[8,2,16,64,128]{4,3,2,1,0:T(8,128)(2,1)} %copy.13), calls=%async_computation.1 | async-start | bytes 8388608 | tf_op jit(solution)/shard_map/all_to_all | solution.py:38
Sparse Core Ops, SparseCore 0:
  13.6 41.4 all-gather.2

commit v2 on v0

--- a/solution.py
+++ b/solution.py
@@ -3,6 +3,7 @@
 from jax import lax
 from jax.sharding import Mesh
 from jax.sharding import PartitionSpec as P
+from jax.lax import all_to_all, axis_size
 
 ZERO = ("zero_0", "zero_1")
 UNIT_ZERO = ("unit", "zero_0", "zero_1")
@@ -45,7 +46,10 @@
         scale_down, lax.axis_index(ZERO) * ready_down.shape[1], ready_down.shape[1], axis=1
     )
     part_router = (router_weight * router_gain[:, None]).astype(jnp.bfloat16)
-    row_router = lax.all_gather(part_router, ZERO, axis=0, tiled=True)
+    y1 = axis_size(ZERO)
+    v1 = jnp.stack(y1 * [part_router], axis=0)
+    u1 = all_to_all(v1, ZERO, 0, 0)
+    row_router = jnp.concatenate(u1, 0)
     serve_router = lax.all_gather(row_router, "bank", axis=1, tiled=True)
     return (ready_down, scale_down, serve_router)
 

time: 209 us -> 200 us (0.957)
  blocking collectives: 124 us -> 20.7 us
  waiting for transfers between devices: 41.7 us -> 128 us
  starting transfers between devices: 4.71 us -> 9.25 us
  local copies, waits for them, and re-layouts: 11.6 us -> 14.8 us
    all_gather x1 -> x0, blocking collectives: 104 us -> none  [per_device(): row_router = lax.all_gather(part_router, ZERO, axis=0, tiled=True)]
    all_to_all x1, waiting for transfers between devices: 0.01 us -> 83.6 us  [turned_blocks(): lax.all_to_all(tiles, axes[k], split_axis=k, concat_axis=k, tiled=True)]
    all_to_all x0 -> x1, starting transfers between devices: none -> 4.36 us  [per_device(): u1 = all_to_all(v1, ZERO, 0, 0)]
    all_to_all x1, local copies, waits for them, and re-layouts: 2.97 us -> 5.52 us  [turned_blocks(): lax.all_to_all(tiles, axes[k], split_axis=k, concat_axis=k, tiled=True)]
    all_to_all x0 -> x1, waiting for transfers between devices: none -> 2.27 us  [per_device(): u1 = all_to_all(v1, ZERO, 0, 0)]
  transfers between devices with their start and end apart: 2 -> 3, of which waited for: 1 -> 3; matrix products, arithmetic and copies ran while one was open for 0% -> 3% of each run, Pallas kernels for 0% -> 0%
where the time goes in v2:
time: 200 us; the launch traced here: 199 us
  waiting for transfers between devices  128 us (64%)
  blocking collectives  20.7 us (10%)
  local copies, waits for them, and re-layouts  14.8 us (7%)
  between operations  14.2 us (7%)
  other arithmetic  12.8 us (6%)
  starting transfers between devices  9.25 us (5%)
    all_to_all x1, waiting for transfers between devices, turned_blocks(): lax.all_to_all(tiles, axes[k], split_axis=k, concat_axis=k, tiled=True)  83.6 us
    all_gather x1, waiting for transfers between devices, gathered_total(): tiles = lax.all_gather(value, axis)  41.6 us
    all_gather x1, blocking collectives, per_device(): serve_router = lax.all_gather(row_router, 'bank', axis=1, tiled=True)  12.5 us
    all_to_all x1, blocking collectives, turned_blocks(): lax.all_to_all(tiles, axes[k], split_axis=k, concat_axis=k, tiled=True)  8.15 us
    reduce_max x1, other arithmetic, per_device(): scale_down = gathered_total(jnp.max(jnp.abs(train_down), axis=2), ZERO)  6.25 us
    all_to_all x1, local copies, waits for them, and re-layouts, turned_blocks(): lax.all_to_all(tiles, axes[k], split_axis=k, concat_axis=k, tiled=True)  5.52 us
    reshape x1, local copies, waits for them, and re-layouts, joined_along(): tiles.reshape(*dims[:dim], dims[dim] * dims[dim + 1], *dims[dim + 2:])  5.35 us
    convert_element_type x1, other arithmetic, per_device(): (train_down / jnp.expand_dims(scale_down, 2)).astype(jnp.bfloat16)  5.26 us
  transfers between devices with their start and end apart: 3, of which 3 were waited for; matrix products, arithmetic and copies ran while one was open for 3% of the time, Pallas kernels for 0%

profile of v2, /device:TPU:2, one launch (start us, length us, event | category | flops | bytes accessed | tf_op | source)
XLA Modules:
  0.0 199.2 jit_solution(2524754201618451619)
XLA Ops:
  7.2 0.0 copy-start
  7.2 0.0 copy-start.1
  7.2 0.0 all-gather.3.cloned.1.call-start
  7.2 6.2 %abs_reduce_fusion = f32[16,1024]{1,0:T(8,128)} fusion(f32[16,1024,128]{2,1,0:T(8,128)} %param.3), kind=kLoop, calls=%fused_computation.1 | loop fusion | flops 4177920 | bytes 8454144 | tf_op jit(solution)/shard_map/reduce_max | solution.py:42
  13.5 0.0 all-gather.3.cloned.1.call-update
  13.5 0.0 copy-done
  13.5 0.0 copy-done.1
  13.5 41.6 %all-gather.3.cloned.1.call-done = f32[256,1024]{1,0:T(8,128)} async-done(((f32[16,1024]{1,0:T(8,128)}), f32[256,1024]{1,0:T(8,128)}) %all-gather.3.cloned.1.call-update) | async-done | bytes 1048592 | tf_op jit(solution)/shard_map/all_gather | solution.py:13
  55.2 1.3 reduce_max.19
  56.5 5.3 %divide_convert_fusion = bf16[16,1024,128]{2,1,0:T(8,128)(2,1)S(1)} fusion(f32[16,1024,128]{2,1,0:T(8,128)} %param.3, f32[16,1024]{1,0:T(8,128)S(1)} %reduce_max.19), kind=kLoop, calls=%fused_computation | loop fusion | flops 4194304 | bytes 12648448 | tf_op jit(solution)/shard_map/convert_element_type | solution.py:43
  62.4 1.3 copy.14
  63.7 8.2 %all_to_all.15 = bf16[8,2,16,64,128]{4,3,2,0,1:T(8,128)(2,1)} all-to-all(bf16[8,2,16,64,128]{4,3,2,0,1:T(8,128)(2,1)S(1)} %copy.14), channel_id=1, replica_groups=mesh['unit'=4,'bank'=4,'zero_0'=8,'zero_1'=2] {'zero_1'}, dimensions={1} | all-to-all | bytes 8388608 | tf_op jit(solution)/shard_map/all_to_all | solution.py:31
  71.9 0.6 stack.87
  72.5 4.4 %all-to-all-start.2 = ((bf16[16,128,16]{1,2,0:T(8,128)(2,1)}), bf16[16,128,16]{1,2,0:T(8,128)(2,1)S(1)}, u32[]{:S(2)}, u32[]{:S(2)}) async-start(bf16[16,128,16]{1,2,0:T(8,128)(2,1)} %stack.87), calls=%async_computation.2 | async-start | bytes 131072 | tf_op jit(solution)/shard_map/all_to_all | solution.py:51
  76.9 5.5 %copy.15 = bf16[8,2,16,64,128]{4,3,2,1,0:T(8,128)(2,1)} copy(bf16[8,2,16,64,128]{4,3,2,0,1:T(8,128)(2,1)} %all_to_all.15) | data formatting | bytes 8388608 | tf_op jit(solution)/shard_map/all_to_all | solution.py:31
  82.4 2.3 %all-to-all-done.2 = bf16[16,128,16]{1,2,0:T(8,128)(2,1)S(1)} async-done(((bf16[16,128,16]{1,2,0:T(8,128)(2,1)}), bf16[16,128,16]{1,2,0:T(8,128)(2,1)S(1)}, u32[]{:S(2)}, u32[]{:S(2)}) %all-to-all-start.2) | async-done | bytes 65568 | tf_op jit(solution)/shard_map/all_to_all | solution.py:51
  84.7 4.8 %all-to-all-start.1 = ((bf16[8,2,16,64,128]{4,3,2,1,0:T(8,128)(2,1)}), bf16[8,2,16,64,128]{4,3,2,1,0:T(8,128)(2,1)}, u32[]{:S(2)}, u32[]{:S(2)}) async-start(bf16[8,2,16,64,128]{4,3,2,1,0:T(8,128)(2,1)} %copy.15), calls=%async_computation.1 | async-start | bytes 8388608 | tf_op jit(solution)/shard_map/all_to_all | solution.py:31
  89.5 12.5 %all_gather.11 = bf16[2048,64]{0,1:T(8,128)(2,1)S(1)} all-gather(bf16[2048,16]{0,1:T(8,128)(2,1)S(1)} %copy_bitcast_fusion.1), channel_id=1, replica_groups=mesh['unit'=4,'bank'=4,'zero_0'=8,'zero_1'=2] {'bank'}, dimensions={1}, use_global_device_ids=true | all-gather | bytes 327680 | tf_op jit(solution)/shard_map/all_gather | solution.py:53
  102.0 0.7 constant_dynamic-slice_fusion
  102.7 83.6 %all-to-all-done.1 = bf16[8,2,16,64,128]{4,3,2,1,0:T(8,128)(2,1)} async-done(((bf16[8,2,16,64,128]{4,3,2,1,0:T(8,128)(2,1)}), bf16[8,2,16,64,128]{4,3,2,1,0:T(8,128)(2,1)}, u32[]{:S(2)}, u32[]{:S(2)}) %all-to-all-start.1) | async-done | bytes 4194336 | tf_op jit(solution)/shard_map/all_to_all | solution.py:31
  186.3 5.3 %copy.22 = bf16[16,16,8,8,128]{4,3,0,2,1:T(8,128)(2,1)} copy(bf16[16,16,8,8,128]{4,3,2,1,0:T(8,128)(2,1)} %bitcast.21) | data formatting | bytes 8388608 | tf_op jit(solution)/shard_map/reshape | solution.py:24
  191.7 0.7 copy.39
  (18 shorter events, 0.6 us)
Async XLA Ops:
  7.2 6.3 %copy-start = (f32[128,16]{0,1:T(8,128)S(1)}, f32[128,16]{0,1:T(8,128)}, u32[]{:S(2)}) copy-start(f32[128,16]{0,1:T(8,128)} %param.4) | copy-start | bytes 24580
  7.2 6.3 %copy-start.1 = (f32[128]{0:T(128)S(1)}, f32[128]{0:T(128)}, u32[]{:S(2)}) copy-start(f32[128]{0:T(128)} %param.5) | copy-start | bytes 1540
  7.2 48.0 %all-gather.3.cloned.1.call-start = ((), (), s32[]{:S(2)}) async-start(), calls=%async_computation.3 | async-start | bytes 1114112 | tf_op jit(solution)/shard_map/all_gather | solution.py:13
  72.5 12.2 %all-to-all-start.2 = ((bf16[16,128,16]{1,2,0:T(8,128)(2,1)}), bf16[16,128,16]{1,2,0:T(8,128)(2,1)S(1)}, u32[]{:S(2)}, u32[]{:S(2)}) async-start(bf16[16,128,16]{1,2,0:T(8,128)(2,1)} %stack.87), calls=%async_computation.2 | async-start | bytes 131072 | tf_op jit(solution)/shard_map/all_to_all | solution.py:51
  84.7 101.7 %all-to-all-start.1 = ((bf16[8,2,16,64,128]{4,3,2,1,0:T(8,128)(2,1)}), bf16[8,2,16,64,128]{4,3,2,1,0:T(8,128)(2,1)}, u32[]{:S(2)}, u32[]{:S(2)}) async-start(bf16[8,2,16,64,128]{4,3,2,1,0:T(8,128)(2,1)} %copy.15), calls=%async_computation.1 | async-start | bytes 8388608 | tf_op jit(solution)/shard_map/all_to_all | solution.py:31
Sparse Core Ops, SparseCore 0:
  13.6 41.4 all-gather.2
